TPU v7x, 32 devices: a whole 2x2x4 slice. The times are simulated.
32 devices in a mesh: blk: 8 (over z, y), sub: 4 (over x, core).
Axes of the slice: x: 2, y: 2, z: 4, core: 2. Of those that a mesh axis runs over, the one named last changes fastest.
Arguments:
- integrals: float32 [32, 4, 32, 6144], P('blk', 'sub'), may hold values from -1 to 1
- slot_order: int32 [32, 4, 32], P('blk', 'sub'), may hold values from 0 to 31, each once within a row
- factor_rows: float32 [32, 4, 32, 4096], P(None, 'sub'), may hold values from -1 to 1.5, as said below
- occ_energy: float32 [384], replicated, may hold values from -1.5 to -0.3
- slab_index: int32 [1], replicated, may hold values from 0 to 127
- virt_energy: float32 [2048], replicated, may hold values from 0.1 to 3
Outputs:
- amplitudes: float32 [6144, 6144], P('blk', 'sub')
Inputs may be any that keep to these rules, and one draw needn't show every extreme that they name: `slot_order`: each row of 32 entries holds every number from 0 to 31 once. `factor_rows`: the factor is lower triangular (zero above its diagonal) with diagonal entries between 0.5 and 1.5.
All inputs are finite; a program needn't handle non-finite values.
Results may differ from a plain program's by a relative error of at most 0.0001.
Values sent between devices are 32-bit elements; how exact they have to be, the bound alone decides.
A program may use at most 128 MiB of HBM per device.

v0:
```python
import jax
import jax.numpy as jnp
from jax import lax
from jax.sharding import PartitionSpec as P

NVIRT = 2048
NOCC = 3
PRECISE = lax.Precision.HIGHEST


def canonical_order(integrals, slot_order):
    piece_len = integrals.shape[2]
    places = jnp.arange(piece_len, dtype=jnp.int32)
    onehot = (slot_order[..., None] == places).astype(jnp.float32)
    return jnp.einsum("rscq,rscp->rsqp", onehot, integrals, precision=PRECISE)


def transposed_dot(left, right):
    return lax.dot_general(left, right, (((0,), (0,)), ((), ())), precision=PRECISE)


def after_section(solved, own_rows, rhs_rows, diag_inverse, first, reach):
    round_width = diag_inverse.shape[1]
    pair_cols = solved.shape[2]
    width = reach * round_width
    rows_part = own_rows[:, :, :width]

    def advance(round_id, solved):
        factor_part = lax.dynamic_index_in_dim(rows_part, round_id, 0, keepdims=False)
        known_part = jnp.dot(
            factor_part, solved[:reach].reshape(width, pair_cols), precision=PRECISE
        )
        updated = lax.dynamic_index_in_dim(rhs_rows, round_id, 0, keepdims=False) - known_part
        round_block = lax.all_gather(updated[None], "sub", axis=0, tiled=True).reshape(
            round_width, pair_cols
        )
        inverse = lax.dynamic_index_in_dim(diag_inverse, round_id, 0, keepdims=False)
        solved_round = jnp.dot(inverse, round_block, precision=PRECISE)
        return lax.dynamic_update_index_in_dim(solved, solved_round, round_id, 0)

    return lax.fori_loop(first, reach, advance, solved, unroll=True)


def shards(integrals, slot_order, factor_rows, occ_energy, slab_index, virt_energy):
    canonical = canonical_order(integrals, slot_order)
    local_rhs = lax.all_to_all(canonical, "blk", split_axis=3, concat_axis=0, tiled=True)
    rounds = factor_rows.shape[0]
    piece_len = factor_rows.shape[2]
    sub_count = lax.axis_size("sub")
    round_width = sub_count * piece_len
    pair_cols = local_rhs.shape[3]
    shaped = factor_rows.reshape(rounds, piece_len, rounds, round_width)
    round_ids = jnp.arange(rounds)
    own_diag = shaped[round_ids, :, round_ids, :]
    diag_blocks = lax.all_gather(own_diag[:, None], "sub", axis=1, tiled=True).reshape(
        rounds, round_width, round_width
    )
    identity = jnp.broadcast_to(
        jnp.eye(round_width, dtype=jnp.float32), (rounds, round_width, round_width)
    )
    diag_inverse = jax.scipy.linalg.solve_triangular(diag_blocks, identity, lower=True)
    rhs_rows = local_rhs[:, 0]
    own_rows = factor_rows[:, 0]
    solved_start = jnp.zeros((rounds, round_width, pair_cols), jnp.float32)
    section_count = min(8, rounds)
    per_section = rounds // section_count
    solved = solved_start
    for section_id in range(section_count):
        solved = after_section(
            solved,
            own_rows,
            rhs_rows,
            diag_inverse,
            section_id * per_section,
            (section_id + 1) * per_section,
        )
    sub_index = lax.axis_index("sub")
    total_pairs = pair_cols * lax.axis_size("blk")
    quarter = total_pairs // sub_count
    solved_full = solved.reshape(rounds, sub_count, piece_len, pair_cols)
    own_part = lax.dynamic_index_in_dim(solved_full, sub_index, 1, keepdims=False).reshape(
        rounds * piece_len, pair_cols
    )
    product = transposed_dot(own_part, lax.all_gather(own_part, "blk", axis=1, tiled=True))
    coulomb = lax.psum_scatter(product, "sub", scatter_dimension=1, tiled=True)
    slab_start = slab_index[0] * NOCC
    occ_slab = lax.dynamic_slice_in_dim(occ_energy, slab_start, NOCC)
    pair_energy = jnp.repeat(occ_slab, NVIRT) - jnp.tile(virt_energy, NOCC)
    row_energy = lax.dynamic_slice_in_dim(pair_energy, lax.axis_index("blk") * pair_cols, pair_cols)
    col_energy = lax.dynamic_slice_in_dim(pair_energy, sub_index * quarter, quarter)
    return coulomb / (row_energy[:, None] + col_energy[None, :])


def solution(mesh):
    in_specs = (
        P("blk", "sub", None, None),
        P("blk", "sub", None),
        P(None, "sub", None, None),
        P(),
        P(),
        P(),
    )
    out_specs = P("blk", "sub")
    return jax.shard_map(shards, mesh=mesh, in_specs=in_specs, out_specs=out_specs, check_vma=False)
```

profile of v0, /device:TPU:0, one launch (start us, length us, event | category | flops | bytes accessed | tf_op | source)
XLA Modules:
  0.0 1643.7 jit_solution(12217533241742672340)
XLA Ops:
  12.4 10.1 copy.18
  22.5 12.3 reshape.389
  34.8 7.3 all-to-all-start
  42.1 9.4 copy.23
  51.5 13.8 copy.16
  65.3 7.2 gather_fusion
  73.5 23.0 %all-gather.37.cloned.1.call-done = f32[32,128,128]{2,1,0:T(8,128)} async-done(((f32[32,32,128]{2,1,0:T(8,128)}), f32[32,128,128]{2,1,0:T(8,128)}) %all-gather.37.cloned.1.call-update) | async-done | bytes 2097168 | tf_op jit(solution)/shard_map/all_gather | solution.py:55
  99.7 315.9 %custom-call.4 = f32[32,1,128,128]{2,3,1,0:T(8,128)} custom-call(f32[32,1,128,128]{3,2,1,0:T(8,128)} %bitcast_select_fusion), custom_call_target="InvertDiagBlocksLowerTriangular" | custom-call | tf_op jit(solution)/shard_map/jit(_solve_triangular)/vmap()/triangular_solve | solution.py:61
  422.6 11.4 reduce.8
  434.0 13.0 reshape.390
  447.0 7.6 copy.22
  465.5 7.0 all-gather.1
  509.4 6.7 all-gather.5
  520.7 6.6 all-gather.6
  543.9 6.8 all-gather.8
  580.2 7.0 all-gather.11
  607.5 6.7 all-gather.13
  621.0 6.6 all-gather.14
  634.5 6.8 all-gather.15
  663.6 7.0 all-gather.17
  678.5 6.6 all-gather.18
  692.9 6.7 all-gather.19
  705.5 7.3 fusion.48
  712.9 6.6 all-gather.20
  725.3 7.3 fusion.47
  732.6 6.6 all-gather.21
  745.1 7.3 fusion.46
  764.8 7.3 fusion.45
  772.2 6.8 all-gather.23
  785.7 10.9 fusion.44
  796.6 6.8 all-gather.24
  810.1 10.9 fusion.43
  821.0 7.0 all-gather.25
  834.8 10.9 fusion.42
  845.7 6.7 all-gather.26
  859.1 10.9 fusion.41
  870.0 6.8 all-gather.27
  878.1 8.6 fusion.40
  886.7 6.8 all-gather.28
  894.9 8.6 fusion.39
  903.5 7.0 all-gather.29
  911.8 8.6 fusion.38
  920.5 6.7 all-gather.30
  928.5 8.6 fusion.37
  937.1 6.6 all-gather.31
  947.1 480.5 %all-gather.35.cloned.1.call-done = f32[1024,6144]{1,0:T(8,128)} async-done(((f32[1024,768]{1,0:T(8,128)}), f32[1024,6144]{1,0:T(8,128)}) %all-gather.35.cloned.1.call-update) | async-done | bytes 25165840 | tf_op jit(solution)/shard_map/all_gather | solution.py:84
  1427.6 66.3 %fusion.77 = f32[768,6144]{1,0:T(8,128)} fusion(f32[1024,768]{1,0:T(8,128)} %bitcast.777, f32[1024,6144]{1,0:T(8,128)} %all-gather.35.cloned.1.call-done), kind=kOutput, calls=%fused_computation.243 | convolution fusion | flops 57982058496 | bytes 47185920 | tf_op jit(solution)/shard_map/dot_general | solution.py:19
  1495.9 135.9 %reduce-scatter.2.cloned.1.call-done = f32[768,1536]{1,0:T(8,128)} async-done(((f32[768,6144]{1,0:T(8,128)}), f32[768,1536]{1,0:T(8,128)}) %reduce-scatter.2.cloned.1.call-update) | async-done | bytes 4718608 | tf_op jit(solution)/shard_map/reduce_scatter | solution.py:85
  (121 shorter events, 259.1 us)
Async XLA Ops:
  6.5 1.9 copy-start
  34.8 387.3 %all-to-all-start = ((f32[8,1,98304]{2,1,0:T(1,128)}), f32[8,1,98304]{2,1,0:T(1,128)S(1)}, u32[]{:S(2)}, u32[]{:S(2)}) async-start(f32[8,1,98304]{2,1,0:T(1,128)} %reshape.389), calls=%async_computation | async-start | bytes 6291456 | tf_op jit(solution)/shard_map/all_to_all | solution.py:46
  42.1 54.5 %all-gather.37.cloned.1.call-start = ((), (), s32[]{:S(2)}) async-start(), calls=%async_computation.4 | async-start | bytes 2621440 | tf_op jit(solution)/shard_map/all_gather | solution.py:55
  72.5 1355.1 %all-gather.35.cloned.1.call-start = ((), (), s32[]{:S(2)}) async-start(), calls=%async_computation.2 | async-start | bytes 28311552 | tf_op jit(solution)/shard_map/all_gather | solution.py:84
  455.6 309.2 %copy-start.2 = (f32[8,4,1,32,768]{4,3,1,0,2:T(8,128)}, f32[8,4,1,32,768]{4,3,1,0,2:T(8,128)S(1)}, u32[]{:S(2)}) copy-start(f32[8,4,1,32,768]{4,3,1,0,2:T(8,128)S(1)} %copy.20) | copy-start | bytes 9437188
  947.1 684.7 %reduce-scatter.2.cloned.1.call-start = ((), (), s32[]{:S(2)}) async-start(), calls=%async_computation.3 | async-start | bytes 23592960 | tf_op jit(solution)/shard_map/reduce_scatter | solution.py:85
  1493.9 1.7 copy-start.3
  1493.9 143.0 %copy-start.1 = (f32[4,1,32,6144]{3,2,1,0:T(8,128)S(1)}, f32[4,1,32,6144]{3,2,1,0:T(8,128)}, u32[]{:S(2)}) copy-start(f32[4,1,32,6144]{3,2,1,0:T(8,128)} %param.6) | copy-start | bytes 9437188
Sparse Core Ops, SparseCore 0:
  72.6 23.9 all-gather.36
  947.2 480.3 all-gather.34
  1494.1 137.6 reduce-scatter.1
where the time goes:
time: 1650 us; the launch traced here: 1640 us
  waiting for transfers between devices  639 us (39%)
  other arithmetic  337 us (20%)
  matrix products  301 us (18%)
  blocking collectives  214 us (13%)
  local copies, waits for them, and re-layouts  130 us (8%)
    all_gather x1, waiting for transfers between devices, shards(): lax.all_gather(own_part, 'blk', axis=1, tiled=True)  480 us
    another operation x3, other arithmetic, shards(): jax.scipy.linalg.solve_triangular(diag_blocks, identity, lower=True)  319 us
    all_gather x32, blocking collectives, advance(): lax.all_gather(updated[None], 'sub', axis=0, tiled=True)  214 us
    dot_general x31, matrix products, advance(): jnp.dot(factor_part, solved[:reach].reshape(width, pair_cols), precision=...  182 us
    reduce_scatter x1, waiting for transfers between devices, shards(): coulomb = lax.psum_scatter(product, 'sub', scatter_dimension=1, tiled=True)  136 us
    dot_general x1, matrix products, transposed_dot(): lax.dot_general(left, right, (((0,), (0,)), ((), ())), precision=PRECISE)  66.3 us
    slice x27, local copies, waits for them, and re-layouts, advance(): solved[:reach].reshape(width, pair_cols)  48.7 us
    dot_general x32, matrix products, advance(): solved_round = jnp.dot(inverse, round_block, precision=PRECISE)  42 us
  transfers between devices with their start and end apart: 4, of which 3 were waited for; matrix products, arithmetic and copies ran while one was open for 22% of the time, Pallas kernels for 0%

commit v1 on v0

--- a/solution.py
+++ b/solution.py
@@ -1,3 +1,4 @@
+import functools
 import jax
 import jax.numpy as jnp
 from jax import lax
@@ -6,6 +7,15 @@
 NVIRT = 2048
 NOCC = 3
 PRECISE = lax.Precision.HIGHEST
+
+
+def link_surface_all(mine, bus_axis):
+    spare = lax.all_gather(mine, bus_axis)
+    r1 = jnp.concatenate(spare, 1)
+    return r1
+
+
+feed_rails = functools.partial(link_surface_all, bus_axis="blk")
 
 
 def canonical_order(integrals, slot_order):
@@ -81,7 +91,7 @@
     own_part = lax.dynamic_index_in_dim(solved_full, sub_index, 1, keepdims=False).reshape(
         rounds * piece_len, pair_cols
     )
-    product = transposed_dot(own_part, lax.all_gather(own_part, "blk", axis=1, tiled=True))
+    product = transposed_dot(own_part, feed_rails(own_part))
     coulomb = lax.psum_scatter(product, "sub", scatter_dimension=1, tiled=True)
     slab_start = slab_index[0] * NOCC
     occ_slab = lax.dynamic_slice_in_dim(occ_energy, slab_start, NOCC)

time: 1650 us -> 1740 us (1.055)
  matrix products: 301 us -> 357 us
  local copies, waits for them, and re-layouts: 130 us -> 155 us
    dot_general x1, matrix products: 66.3 us -> 122 us  [transposed_dot(): lax.dot_general(left, right, (((0,), (0,)), ((), ())), precision=PRECISE)]
    all_gather x0 -> x1, local copies, waits for them, and re-layouts: none -> 24.7 us  [link_surface_all(): spare = lax.all_gather(mine, bus_axis)]
    unnamed x11 -> x13, local copies, waits for them, and re-layouts: 36.6 us -> 36.6 us
  transfers between devices with their start and end apart: 4 -> 4, of which waited for: 3 -> 3; matrix products, arithmetic and copies ran while one was open for 22% -> 21% of each run, Pallas kernels for 0% -> 0%
where the time goes in v1:
time: 1740 us; the launch traced here: 1720 us
  waiting for transfers between devices  639 us (37%)
  matrix products  357 us (21%)
  other arithmetic  337 us (19%)
  blocking collectives  214 us (12%)
  local copies, waits for them, and re-layouts  155 us (9%)
    all_gather x1, waiting for transfers between devices, link_surface_all(): spare = lax.all_gather(mine, bus_axis)  480 us
    another operation x3, other arithmetic, shards(): jax.scipy.linalg.solve_triangular(diag_blocks, identity, lower=True)  319 us
    all_gather x32, blocking collectives, advance(): lax.all_gather(updated[None], 'sub', axis=0, tiled=True)  214 us
    dot_general x31, matrix products, advance(): jnp.dot(factor_part, solved[:reach].reshape(width, pair_cols), precision=...  182 us
    reduce_scatter x1, waiting for transfers between devices, shards(): coulomb = lax.psum_scatter(product, 'sub', scatter_dimension=1, tiled=True)  136 us
    dot_general x1, matrix products, transposed_dot(): lax.dot_general(left, right, (((0,), (0,)), ((), ())), precision=PRECISE)  122 us
    slice x27, local copies, waits for them, and re-layouts, advance(): solved[:reach].reshape(width, pair_cols)  48.6 us
    dot_general x32, matrix products, advance(): solved_round = jnp.dot(inverse, round_block, precision=PRECISE)  42 us
  transfers between devices with their start and end apart: 4, of which 3 were waited for; matrix products, arithmetic and copies ran while one was open for 21% of the time, Pallas kernels for 0%

profile of v1, /device:TPU:0, one launch (start us, length us, event | category | flops | bytes accessed | tf_op | source)
XLA Modules:
  0.0 1723.9 jit_solution(14020297798425372031)
XLA Ops:
  12.4 10.0 copy.23
  22.4 12.3 reshape.398
  34.7 7.3 all-to-all-start
  42.1 9.4 copy.31
  51.5 13.7 copy.21
  65.2 7.2 gather_fusion
  73.5 23.0 %all-gather.37.cloned.1.call-done = f32[32,128,128]{2,1,0:T(8,128)} async-done(((f32[32,32,128]{2,1,0:T(8,128)}), f32[32,128,128]{2,1,0:T(8,128)}) %all-gather.37.cloned.1.call-update) | async-done | bytes 2097168 | tf_op jit(solution)/shard_map/all_gather | solution.py:65
  99.7 315.9 %custom-call.4 = f32[32,1,128,128]{2,3,1,0:T(8,128)} custom-call(f32[32,1,128,128]{3,2,1,0:T(8,128)} %bitcast_select_fusion), custom_call_target="InvertDiagBlocksLowerTriangular" | custom-call | tf_op jit(solution)/shard_map/jit(_solve_triangular)/vmap()/triangular_solve | solution.py:71
  422.4 11.2 reduce.8
  433.7 13.0 reshape.399
  446.7 7.6 copy.29
  465.2 7.0 all-gather.1
  476.9 6.6 all-gather.2
  509.1 6.7 all-gather.5
  520.4 6.6 all-gather.6
  543.6 6.8 all-gather.8
  567.9 6.6 all-gather.10
  579.9 7.0 all-gather.11
  607.2 6.7 all-gather.13
  620.7 6.6 all-gather.14
  634.1 6.8 all-gather.15
  663.3 7.0 all-gather.17
  692.6 6.7 all-gather.19
  705.2 7.3 fusion.48
  725.0 7.3 fusion.47
  732.3 6.6 all-gather.21
  744.8 7.3 fusion.46
  764.5 7.3 fusion.45
  771.9 6.8 all-gather.23
  785.4 10.9 fusion.44
  796.3 6.8 all-gather.24
  809.8 10.9 fusion.43
  820.7 7.0 all-gather.25
  834.4 10.9 fusion.42
  845.3 6.7 all-gather.26
  858.8 10.9 fusion.41
  869.7 6.8 all-gather.27
  877.8 8.6 fusion.40
  886.4 6.8 all-gather.28
  894.5 8.6 fusion.39
  903.2 7.0 all-gather.29
  911.5 8.6 fusion.38
  920.1 6.7 all-gather.30
  928.2 8.6 fusion.37
  946.8 480.5 %all-gather.35.cloned.1.call-done = f32[8,1024,768]{2,1,0:T(8,128)} async-done(((f32[1,1024,768]{2,1,0:T(8,128)}), f32[8,1024,768]{2,1,0:T(8,128)}) %all-gather.35.cloned.1.call-update) | async-done | bytes 25165840 | tf_op jit(solution)/shard_map/all_gather | solution.py:13
  1427.3 24.7 %copy.27 = f32[8,1024,768]{1,2,0:T(8,128)} copy(f32[8,1024,768]{2,1,0:T(8,128)} %all-gather.35.cloned.1.call-done) | data formatting | bytes 50331648 | tf_op jit(solution)/shard_map/all_gather | solution.py:13
  1452.0 122.0 %fusion.77 = f32[768,6144]{1,0:T(8,128)} fusion(f32[1024,768]{1,0:T(8,128)S(1)} %bitcast.785, f32[1024,6144]{0,1:T(8,128)} %bitcast.743), kind=kOutput, calls=%fused_computation.243 | convolution fusion | flops 57982058496 | bytes 47185920 | tf_op jit(solution)/shard_map/dot_general | solution.py:29
  1576.0 135.9 %reduce-scatter.2.cloned.1.call-done = f32[768,1536]{1,0:T(8,128)} async-done(((f32[768,6144]{1,0:T(8,128)}), f32[768,1536]{1,0:T(8,128)}) %reduce-scatter.2.cloned.1.call-update) | async-done | bytes 4718608 | tf_op jit(solution)/shard_map/reduce_scatter | solution.py:95
  (124 shorter events, 265.5 us)
Async XLA Ops:
  6.5 1.9 copy-start
  34.7 387.2 %all-to-all-start = ((f32[8,1,98304]{2,1,0:T(1,128)}), f32[8,1,98304]{2,1,0:T(1,128)S(1)}, u32[]{:S(2)}, u32[]{:S(2)}) async-start(f32[8,1,98304]{2,1,0:T(1,128)} %reshape.398), calls=%async_computation | async-start | bytes 6291456 | tf_op jit(solution)/shard_map/all_to_all | solution.py:56
  42.0 54.5 %all-gather.37.cloned.1.call-start = ((), (), s32[]{:S(2)}) async-start(), calls=%async_computation.4 | async-start | bytes 2621440 | tf_op jit(solution)/shard_map/all_gather | solution.py:65
  72.4 1354.8 %all-gather.35.cloned.1.call-start = ((), (), s32[]{:S(2)}) async-start(), calls=%async_computation.2 | async-start | bytes 28311552 | tf_op jit(solution)/shard_map/all_gather | solution.py:13
  455.3 309.2 %copy-start.2 = (f32[8,4,1,32,768]{4,3,1,0,2:T(8,128)}, f32[8,4,1,32,768]{4,3,1,0,2:T(8,128)S(1)}, u32[]{:S(2)}) copy-start(f32[8,4,1,32,768]{4,3,1,0,2:T(8,128)S(1)} %copy.25) | copy-start | bytes 9437188
  946.7 505.2 %copy-start.3 = (f32[32,1,32,768]{3,2,1,0:T(8,128)S(1)}, f32[32,1,32,768]{3,2,1,0:T(8,128)}, u32[]{:S(2)}) copy-start(f32[32,1,32,768]{3,2,1,0:T(8,128)} %constant_dynamic-slice_fusion) | copy-start | bytes 9437188
  946.8 765.1 %reduce-scatter.2.cloned.1.call-start = ((), (), s32[]{:S(2)}) async-start(), calls=%async_computation.3 | async-start | bytes 23592960 | tf_op jit(solution)/shard_map/reduce_scatter | solution.py:95
  1574.0 1.7 copy-start.4
  1574.0 143.0 %copy-start.1 = (f32[4,1,32,6144]{3,2,1,0:T(8,128)S(1)}, f32[4,1,32,6144]{3,2,1,0:T(8,128)}, u32[]{:S(2)}) copy-start(f32[4,1,32,6144]{3,2,1,0:T(8,128)} %param.6) | copy-start | bytes 9437188
Sparse Core Ops, SparseCore 0:
  72.6 23.9 all-gather.36
  946.9 480.3 all-gather.34
  1574.1 137.6 reduce-scatter.1
